TPU v7x, 512 devices: a whole 4x8x8 slice. The times are simulated.
512 devices in a mesh: pool: 16 (over y, core), ga: 32 (over x, z).
Axes of the slice: x: 4, y: 8, z: 8, core: 2. Of those that a mesh axis runs over, the one named last changes fastest.
Arguments:
- coefficients: bfloat16 [16, 1024, 2, 256, 128], P('pool', 'ga'), may hold values from -6 to 6
- stick_count: int32 [16, 32], P('pool', 'ga'), may hold values from 28 to 32, as said below
- dest_device: int32 [16, 1024], P('pool', 'ga'), may hold values from -1 to 31, as said below
- dest_slot: int32 [16, 1024], P('pool', 'ga'), may hold values from -1 to 31, as said below
- source_stick: int32 [16, 1024], P('pool', 'ga'), may hold values from -1 to 1023, as said below
Outputs:
- margins: float32 [16, 2, 256, 256], P('pool', None, 'ga')
Inputs may be any that keep to these rules, and one draw needn't show every extreme that they name: Every k-point has a device whose 32 slots are all live; a device's live sticks are its first stick_count slots. `dest_device`: -1 exactly for sticks that land nowhere (among them all sticks that are not live); no device sends more than 2 of its sticks to one device, and some pair of devices reaches 2 for every k-point. `dest_slot`: -1 where dest_device is -1; the slots named are live slots of the layout of k-point q-1, no slot named twice. `source_stick`: the exact inverse of dest_device and dest_slot: a slot names a stick exactly when that stick names the slot, else -1.
All inputs are finite; a program needn't handle non-finite values.
Results may differ from a plain program's by a relative error of at most 0.0003.
Values may be sent and summed in bfloat16 or wider, within the bound.
A program may use at most 64 MiB of HBM per device.

v0:
```python
import jax
import jax.numpy as jnp
from jax import lax
from jax.sharding import PartitionSpec as P


def split_up(x, dim, devices):
    lengths = x.shape
    pieces = x.reshape(*lengths[:dim], devices, lengths[dim] // devices, *lengths[dim + 1 :])
    return jnp.moveaxis(pieces, dim, 0)


def sent_and_summed(x, axis, dim):
    devices = lax.axis_size(axis)
    pieces = lax.all_to_all(split_up(x, dim, devices), axis, 0, 0, tiled=True)
    return jnp.sum(pieces, axis=0)


def passed_along(value, axis, steps):
    count = lax.axis_size(axis)
    pairs = [(source, (source + steps) % count) for source in range(count)]
    return lax.ppermute(value, axis, pairs)


def margin(bra_rows, ket_rows, slot_count, bands, plane_waves):
    bra_block = bra_rows.reshape(slot_count, 2, bands, plane_waves)
    ket_block = ket_rows.reshape(slot_count, 2, bands, plane_waves)
    swapped = jnp.stack([ket_block[:, 1], -ket_block[:, 0]], axis=1)
    real_part = jnp.einsum(
        "scmg,scng->mn", bra_block, ket_block, preferred_element_type=jnp.float32
    )
    imag_part = jnp.einsum("scmg,scng->mn", bra_block, swapped, preferred_element_type=jnp.float32)
    return jnp.stack([real_part, imag_part])


def owner_rows(partial_value, norm_scale):
    owned = sent_and_summed(partial_value, "ga", 1)
    return owned * norm_scale


def local(coefficients, stick_count, dest_device, dest_slot, source_stick):
    groups = lax.axis_size("ga")
    slot_count = coefficients.shape[1]
    bands = coefficients.shape[3]
    plane_waves = coefficients.shape[4]
    pair_cap = max(2, (2 * slot_count + groups - 1) // groups)
    buffer_rows = groups * pair_cap
    norm_scale = (2 * groups * slot_count * plane_waves) ** (-0.5)
    coef_rows = coefficients.reshape(slot_count, -1)
    slot_list = jnp.arange(slot_count, dtype=jnp.int32)
    buffer_list = jnp.arange(buffer_rows, dtype=jnp.int32)
    live_mask = slot_list < stick_count[0, 0]
    bra_rows = jnp.where(live_mask[:, None], coef_rows, jnp.zeros_like(coef_rows))
    targets = dest_device[0]
    dest_order = dest_slot[0]
    matching = targets[:, None] == targets[None, :]
    earlier = dest_order[None, :] < dest_order[:, None]
    ranking = jnp.sum((matching & earlier).astype(jnp.int32), axis=1)
    position = jnp.where(targets >= 0, targets * pair_cap + ranking, -1)
    packer = (buffer_list[:, None] == position[None, :]).astype(jnp.bfloat16)
    outgoing = jnp.dot(packer, coef_rows, preferred_element_type=jnp.float32).astype(jnp.bfloat16)
    outgoing = outgoing.reshape(groups, pair_cap, -1)
    incoming = lax.all_to_all(outgoing, "ga", split_axis=0, concat_axis=0, tiled=True)
    anchor = source_stick[0]
    source_dev = jnp.where(anchor >= 0, anchor // slot_count, -1)
    matching_in = source_dev[:, None] == source_dev[None, :]
    earlier_in = slot_list[None, :] < slot_list[:, None]
    ranking_in = jnp.sum((matching_in & earlier_in).astype(jnp.int32), axis=1)
    position_in = jnp.where(anchor >= 0, source_dev * pair_cap + ranking_in, -1)
    placer = (position_in[:, None] == buffer_list[None, :]).astype(jnp.bfloat16)
    ket_rows = jnp.dot(
        placer, incoming.reshape(buffer_rows, -1), preferred_element_type=jnp.float32
    ).astype(jnp.bfloat16)
    bra_here = passed_along(bra_rows, "pool", 1)
    partial_value = margin(bra_here, ket_rows, slot_count, bands, plane_waves)
    finished = owner_rows(partial_value, norm_scale)
    result = passed_along(finished, "pool", -1)
    return result[None]


def solution(mesh):
    return jax.shard_map(
        local,
        mesh=mesh,
        in_specs=(
            P("pool", "ga", None, None, None),
            P("pool", "ga"),
            P("pool", "ga"),
            P("pool", "ga"),
            P("pool", "ga"),
        ),
        out_specs=P("pool", None, "ga", None),
        check_vma=False,
    )
```

profile of v0, /device:TPU:1, one launch (start us, length us, event | category | flops | bytes accessed | tf_op | source)
XLA Modules:
  0.0 280.6 jit_solution(4952073619975316441)
XLA Ops:
  0.0 0.0 copy-start.2
  0.0 0.0 copy-start.1
  0.0 5.6 %reshape.86 = bf16[32,65536]{1,0:T(8,128)(2,1)} reshape(bf16[1,32,2,256,128]{4,3,2,1,0:T(8,128)(2,1)} %param.5) | data formatting | bytes 8388608 | tf_op jit(solution)/shard_map/reshape | solution.py:49
  5.6 0.0 copy-done.2
  5.6 0.0 copy-done.1
  5.6 0.2 convert_reduce_fusion
  5.8 7.7 %convolution_convert_fusion = bf16[64,65536]{1,0:T(8,128)(2,1)} fusion(bf16[32,65536]{1,0:T(8,128)(2,1)} %reshape.86, s32[32]{0:T(128)S(1)} %fusion.19), kind=kOutput, calls=%fused_computation | convolution fusion | flops 272631808 | bytes 12583040 | tf_op jit(solution)/shard_map/dot_general | solution.py:61
  13.5 10.6 %reshape.89 = bf16[32,2,65536]{2,1,0:T(2,128)(2,1)} reshape(bf16[64,65536]{1,0:T(8,128)(2,1)} %convolution_convert_fusion) | data formatting | bytes 16777216 | tf_op jit(solution)/shard_map/reshape | solution.py:62
  24.0 13.8 %all-to-all-start = ((bf16[32,2,65536]{2,1,0:T(2,128)(2,1)}), bf16[32,2,65536]{2,1,0:T(2,128)(2,1)}, u32[]{:S(2)}, u32[]{:S(2)}) async-start(bf16[32,2,65536]{2,1,0:T(2,128)(2,1)} %reshape.89), calls=%async_computation | async-start | bytes 16777216 | tf_op jit(solution)/shard_map/all_to_all | solution.py:63
  38.5 0.0 copy-start.3
  38.5 2.5 broadcast_select_fusion
  41.1 2.2 collective-permute-start
  43.2 0.0 copy-done.3
  43.3 0.2 convert_reduce_fusion.1
  43.5 45.2 %collective-permute-done = bf16[32,65536]{1,0:T(8,128)(2,1)S(1)} collective-permute-done((bf16[32,65536]{1,0:T(8,128)(2,1)S(1)}, bf16[32,65536]{1,0:T(8,128)(2,1)S(1)}, u32[]{:S(2)}, u32[]{:S(2)}) %collective-permute-start) | collective-permute-done | bytes 4194336 | tf_op jit(solution)/shard_map/ppermute | solution.py:22
  88.7 2.9 %copy.38 = bf16[4,8,512,128]{3,2,1,0:T(8,128)(2,1)} copy(bf16[4,8,512,128]{3,1,2,0:T(8,128)(2,1)S(1)} %bitcast.69) | data formatting | bytes 8388608
  91.6 134.4 %all-to-all-done = bf16[32,2,65536]{2,1,0:T(2,128)(2,1)} async-done(((bf16[32,2,65536]{2,1,0:T(2,128)(2,1)}), bf16[32,2,65536]{2,1,0:T(2,128)(2,1)}, u32[]{:S(2)}, u32[]{:S(2)}) %all-to-all-start) | async-done | bytes 8388640 | tf_op jit(solution)/shard_map/all_to_all | solution.py:63
  226.0 10.2 %reshape.90 = bf16[64,65536]{1,0:T(8,128)(2,1)} reshape(bf16[32,2,65536]{2,1,0:T(2,128)(2,1)} %all-to-all-done) | data formatting | bytes 16777216 | tf_op jit(solution)/shard_map/reshape | solution.py:72
  236.2 4.7 %fusion.7 = bf16[4,8,512,128]{3,1,2,0:T(8,128)(2,1)S(1)} fusion(bf16[64,65536]{1,0:T(8,128)(2,1)} %reshape.90, s32[32]{0:T(128)S(1)} %compare_select_fusion.8), kind=kOutput, calls=%fused_computation.11 | convolution fusion | flops 270534656 | bytes 12583040 | tf_op jit(solution)/shard_map/dot_general | solution.py:71
  240.9 1.0 copy.39
  241.8 0.0 copy-start
  241.9 0.8 fusion.23
  242.6 1.4 copy-done
  244.0 1.3 fusion.8
  245.3 1.3 fusion.13
  246.7 0.1 copy.33
  246.7 29.2 %all_to_all.10 = f32[32,2,8,256]{3,2,1,0:T(8,128)S(1)} all-to-all(f32[32,2,8,256]{3,2,1,0:T(8,128)S(1)} %copy.33), channel_id=1, replica_groups=mesh['pool'=16,'ga'=32] {'ga'}, dimensions={0} | all-to-all | bytes 1048576 | tf_op jit(solution)/shard_map/all_to_all | solution.py:15
  276.0 3.2 %collective-permute-start.1 = (f32[2,8,256]{2,1,0:T(8,128)S(1)}, f32[2,8,256]{2,1,0:T(8,128)S(1)}, u32[]{:S(2)}, u32[]{:S(2)}) collective-permute-start(f32[2,8,256]{2,1,0:T(8,128)S(1)} %broadcast_multiply_fusion), channel_id=1, source_target_pairs={{0,480},{32,0},{64,32},{96,64},{128,96},{160,128},{192,160},{224,1... | collective-permute-start | bytes 49160 | tf_op jit(solution)/shard_map/ppermute | solution.py:22
  279.2 0.8 collective-permute-done.1
  280.0 0.6 copy.56
  (8 shorter events, 0.1 us)
Async XLA Ops:
  0.0 5.6 %copy-start.2 = (s32[1,32]{1,0:T(1,128)S(1)}, s32[1,32]{1,0:T(1,128)}, u32[]{:S(2)}) copy-start(s32[1,32]{1,0:T(1,128)} %param.7) | copy-start | bytes 388
  0.0 5.6 %copy-start.1 = (s32[1,32]{1,0:T(1,128)S(1)}, s32[1,32]{1,0:T(1,128)}, u32[]{:S(2)}) copy-start(s32[1,32]{1,0:T(1,128)} %param.8) | copy-start | bytes 388
  24.0 201.9 %all-to-all-start = ((bf16[32,2,65536]{2,1,0:T(2,128)(2,1)}), bf16[32,2,65536]{2,1,0:T(2,128)(2,1)}, u32[]{:S(2)}, u32[]{:S(2)}) async-start(bf16[32,2,65536]{2,1,0:T(2,128)(2,1)} %reshape.89), calls=%async_computation | async-start | bytes 16777216 | tf_op jit(solution)/shard_map/all_to_all | solution.py:63
  38.5 4.7 %copy-start.3 = (s32[1,32]{1,0:T(1,128)S(1)}, s32[1,32]{1,0:T(1,128)}, u32[]{:S(2)}) copy-start(s32[1,32]{1,0:T(1,128)} %param.9) | copy-start | bytes 388
  41.1 47.6 %collective-permute-start = (bf16[32,65536]{1,0:T(8,128)(2,1)S(1)}, bf16[32,65536]{1,0:T(8,128)(2,1)S(1)}, u32[]{:S(2)}, u32[]{:S(2)}) collective-permute-start(bf16[32,65536]{1,0:T(8,128)(2,1)S(1)} %broadcast_select_fusion), channel_id=1, source_target_pairs={{0,32},{32,64},{64,96},{96,128},{128,160},{160,192},{192,224},{224... | collective-permute-start | bytes 12582920 | tf_op jit(solution)/shard_map/ppermute | solution.py:22
  241.8 2.2 copy-start
  276.0 4.0 %collective-permute-start.1 = (f32[2,8,256]{2,1,0:T(8,128)S(1)}, f32[2,8,256]{2,1,0:T(8,128)S(1)}, u32[]{:S(2)}, u32[]{:S(2)}) collective-permute-start(f32[2,8,256]{2,1,0:T(8,128)S(1)} %broadcast_multiply_fusion), channel_id=1, source_target_pairs={{0,480},{32,0},{64,32},{96,64},{128,96},{160,128},{192,160},{224,1... | collective-permute-start | bytes 49160 | tf_op jit(solution)/shard_map/ppermute | solution.py:22
where the time goes:
time: 281 us
  waiting for transfers between devices  180 us (64%)
  local copies, waits for them, and re-layouts  32.3 us (11%)
  blocking collectives  29.2 us (10%)
  starting transfers between devices  19.2 us (7%)
  matrix products  15 us (5%)
  other arithmetic  3.79 us (1%)
    all_to_all x1, waiting for transfers between devices, local(): lax.all_to_all(outgoing, 'ga', split_axis=0, concat_axis=0, tiled=True)  134 us
    ppermute x2, waiting for transfers between devices, passed_along(): return lax.ppermute(value, axis, pairs)  46.1 us
    all_to_all x1, blocking collectives, sent_and_summed(): pieces = lax.all_to_all(split_up(x, dim, devices), axis, 0, 0, tiled=True)  29.2 us
    all_to_all x1, starting transfers between devices, local(): lax.all_to_all(outgoing, 'ga', split_axis=0, concat_axis=0, tiled=True)  13.8 us
    reshape x1, local copies, waits for them, and re-layouts, local(): outgoing = outgoing.reshape(groups, pair_cap, -1)  10.6 us
    reshape x1, local copies, waits for them, and re-layouts, local(): incoming.reshape(buffer_rows, -1)  10.2 us
    dot_general x1, matrix products, local(): jnp.dot(packer, coef_rows, preferred_element_type=jnp.float32)  7.72 us
    unnamed x11, local copies, waits for them, and re-layouts  5.87 us
  transfers between devices with their start and end apart: 3, of which 3 were waited for; matrix products, arithmetic and copies ran while one was open for 2% of the time, Pallas kernels for 0%

commit v1 on v0

v1 whole, which is shorter than its diff:
```python
import functools

import jax
import jax.numpy as jnp
from jax import lax
from jax.experimental import pallas as pl
from jax.experimental.pallas import tpu as pltpu
from jax.sharding import PartitionSpec as P

MESH = pl.DeviceIdType.MESH
NX = 4
NZ = 8
WINDOW = 5


def hop_list():
    far = []
    for distance, hop in ((4, 1), (3, 1), (1, 1), (2, 1), (4, 2), (3, 2), (2, 2), (4, 3), (3, 3), (4, 4)):
        far += [(distance, hop, dx) for dx in (2, 1, 3)]
    near = [(d, h, 0) for d, h in ((4, 1), (3, 1), (2, 1), (4, 2), (3, 2), (2, 2), (4, 3), (3, 3), (4, 4), (1, 1))]
    return far + near


HOPS = hop_list()
RELAY = {(2, 1): 0, (3, 1): 1, (3, 2): 2}


def kernel(
    norm_scale,
    pack_ref,
    place_ref,
    count_ref,
    coef_hbm,
    out_ref,
    coef,
    bra,
    count_in,
    packed,
    relay,
    relay_half,
    turn,
    final,
    acc,
    x_in,
    rows,
    z_in,
    load_sem,
    bra_sem,
    count_sem,
    hop_send,
    hop_recv,
    x_send,
    x_recv,
    xr_send,
    xr_recv,
    zr_send,
    zr_recv,
):
    pool = lax.axis_index("pool")
    pools = lax.axis_size("pool")
    ga = lax.axis_index("ga")
    x = ga // NZ
    z = lax.rem(ga, NZ)
    after = lax.rem(pool + 1, pools)
    before = lax.rem(pool + pools - 1, pools)

    def at(dx, dz):
        return lax.rem(x + dx, NX) * NZ + lax.rem(z + dz, NZ)

    load = pltpu.make_async_copy(coef_hbm, coef, load_sem)
    load.start()
    barrier = pltpu.get_barrier_semaphore()
    greeted = [(pool, at(0, 1)), (pool, at(0, NZ - 1))]
    greeted += [(pool, at(dx, 0)) for dx in range(1, NX)]
    greeted += [(before, ga)] + [(after, at(0, dz)) for dz in range(NZ)]
    for device in greeted:
        pl.semaphore_signal(barrier, inc=1, device_id=device, device_id_type=MESH)

    load.wait()

    def pack_unit(unit, carry):
        target = at(lax.rem(unit, NX), unit // NX)
        for rank in range(2):
            packed[unit, rank] = coef[pack_ref[target * 2 + rank]]
        return carry

    lax.fori_loop(0, NX * NZ, pack_unit, 0)
    final[0] = packed[0]
    acc[...] = jnp.zeros_like(acc)
    pl.semaphore_wait(barrier, len(greeted))

    def remote(src, dst, send, recv, device):
        return pltpu.make_async_remote_copy(
            src_ref=src, dst_ref=dst, send_sem=send, recv_sem=recv, device_id=device, device_id_type=MESH
        )

    started = []

    def start(copy):
        copy.start()
        started.append(copy)
        return copy

    def hop_copy(s, n):
        distance, hop, dx = HOPS[n]
        dz = distance if s == 0 else NZ - distance
        unit = dz * NX + dx
        half = distance == NZ // 2
        if hop == 1:
            src = packed.at[unit, s] if half else packed.at[unit]
        elif half:
            src = relay_half.at[s, hop - 2, dx]
        else:
            src = relay.at[s, RELAY[distance, hop - 1], dx]
        if hop < distance:
            dst = relay_half.at[s, hop - 1, dx] if half else relay.at[s, RELAY[distance, hop], dx]
        else:
            dst = final.at[unit] if dx == 0 else turn.at[(dz - 1) * 3 + dx - 1]
            dst = dst.at[s] if half else dst
        return remote(src, dst, hop_send.at[s, n], hop_recv.at[s, n], (pool, at(0, 1 if s == 0 else NZ - 1)))

    hop_copies = [[hop_copy(s, n) for n in range(len(HOPS))] for s in range(2)]

    def x_copy(dz, dx, s):
        unit = dz * NX + dx
        src = packed.at[unit] if dz == 0 else turn.at[(dz - 1) * 3 + dx - 1]
        dst = final.at[unit]
        if dz == NZ // 2:
            src, dst = src.at[s], dst.at[s]
        return remote(src, dst, x_send.at[unit, s], x_recv.at[unit, s], (pool, at(dx, 0)))

    x_copies = {}

    def multiply(first, count, step):
        def one(i, carry):
            unit = first + i * step
            source = lax.rem(x + NX - lax.rem(unit, NX), NX) * NZ + lax.rem(z + NZ - unit // NX, NZ)
            total = None
            for rank in range(2):
                slot = place_ref[source * 2 + rank]
                live = (slot >= 0) & (slot < count_in[0, 0])
                mine = bra[jnp.maximum(slot, 0)]
                mine = jnp.where(live, mine, jnp.zeros_like(mine))
                ket = final[unit, rank]
                ket = jnp.concatenate([ket[:256], ket[256:]], axis=1)
                re, im = mine[:256], mine[256:]
                left = jnp.concatenate(
                    [jnp.concatenate([re, im], axis=1), jnp.concatenate([-im, re], axis=1)], axis=0
                )
                term = lax.dot_general(left, ket, (((1,), (1,)), ((), ())), preferred_element_type=jnp.float32)
                total = term if total is None else total + term
            acc[...] += total.reshape(acc.shape)
            return carry

        lax.fori_loop(0, count, one, 0)

    issued = [0, 0]
    position = {hop: n for n, hop in enumerate(HOPS)}

    def issue(s, arrived):
        while issued[s] < len(HOPS) and issued[s] <= arrived + WINDOW:
            distance, hop, dx = HOPS[issued[s]]
            if hop > 1 and position[distance, hop - 1, dx] > arrived:
                break
            start(hop_copies[s][issued[s]])
            issued[s] += 1

    for s in range(2):
        issue(s, -1)
    bra_copy = start(remote(coef, bra, bra_sem.at[0], bra_sem.at[1], (after, ga)))
    count_copy = start(remote(count_ref, count_in, count_sem.at[0], count_sem.at[1], (after, ga)))
    for dx in (2, 1, 3):
        x_copies[0, dx, 0] = start(x_copy(0, dx, 0))

    def wait_x(*units):
        for key in units:
            x_copies[key].wait_recv()

    three = (2, 1, 3)
    for n, (distance, hop, dx) in enumerate(HOPS):
        for s in range(2):
            hop_copies[s][n].wait_recv()
            if hop == distance and dx != 0:
                dz = distance if s == 0 else NZ - distance
                which = s if distance == NZ // 2 else 0
                x_copies[dz, dx, which] = start(x_copy(dz, dx, which))
            issue(s, n)
        if n == 11:
            bra_copy.wait_recv()
            count_copy.wait_recv()
            wait_x(*[(0, d, 0) for d in three])
            multiply(0, 4, 1)
        if n == 16:
            wait_x(*[(dz, d, 0) for dz in (1, 7) for d in three])
            multiply(5, 3, 1)
            multiply(29, 3, 1)
        if n == 26:
            wait_x(*[(dz, d, 0) for dz in (2, 6) for d in three])
            multiply(9, 3, 1)
            multiply(25, 3, 1)
        if n == 32:
            wait_x(*[(dz, d, 0) for dz in (3, 5) for d in three])
            multiply(13, 3, 1)
            multiply(21, 3, 1)
        if n == 35:
            wait_x(*[(4, d, h) for h in range(2) for d in three])
            multiply(17, 3, 1)
        if n == 37:
            multiply(8, 2, 16)
        if n == 38:
            multiply(12, 3, 4)
    multiply(4, 2, 24)

    sums = []
    for dx in (2, 1, 3):
        theirs = pl.ds(pl.multiple_of(lax.rem(x + dx, NX) * 64, 64), 64)
        sums.append(
            start(
                remote(
                    acc.at[:, theirs], x_in.at[dx - 1], xr_send.at[dx - 1], xr_recv.at[dx - 1], (pool, at(dx, 0))
                )
            )
        )
    for copy in sums:
        copy.wait_recv()
    own = pl.ds(pl.multiple_of(x * 64, 64), 64)
    rows[...] = acc[:, own] + x_in[0] + x_in[1] + x_in[2]
    sums = []
    for dz in (4, 3, 5, 2, 6, 1, 7, 0):
        theirs = pl.ds(pl.multiple_of(lax.rem(z + dz, NZ) * 8, 8), 8)
        sums.append(
            start(remote(rows.at[:, theirs], z_in.at[dz], zr_send.at[dz], zr_recv.at[dz], (before, at(0, dz))))
        )
    for copy in sums:
        copy.wait_recv()
    result = z_in[0]
    for dz in range(1, NZ):
        result = result + z_in[dz]
    out_ref[...] = result * norm_scale
    for copy in started:
        copy.wait_send()


def local(coefficients, stick_count, dest_device, dest_slot, source_stick):
    groups = lax.axis_size("ga")
    slots = coefficients.shape[1]
    bands = coefficients.shape[3]
    waves = coefficients.shape[4]
    norm_scale = (2 * groups * slots * waves) ** (-0.5)
    slot_list = jnp.arange(slots, dtype=jnp.int32)
    row_list = jnp.arange(groups * 2, dtype=jnp.int32)

    def ranked(devices, order):
        same = (devices[:, None] == devices[None, :]) & (order[None, :] < order[:, None])
        rank = jnp.sum(same.astype(jnp.int32), axis=1)
        return jnp.where(devices >= 0, devices * 2 + rank, -1)

    sent = row_list[:, None] == ranked(dest_device[0], dest_slot[0])[None, :]
    pack = jnp.max(jnp.where(sent, slot_list[None, :], 0), axis=1)
    anchor = source_stick[0]
    came = row_list[:, None] == ranked(jnp.where(anchor >= 0, anchor // slots, -1), slot_list)[None, :]
    place = jnp.max(jnp.where(came, slot_list[None, :], -1), axis=1)
    count = jnp.broadcast_to(stick_count, (8, 128))

    stick = (2 * bands, waves)
    bf16, f32 = jnp.bfloat16, jnp.float32
    dma = pltpu.SemaphoreType.DMA
    result = pl.pallas_call(
        functools.partial(kernel, norm_scale),
        out_shape=jax.ShapeDtypeStruct((2, bands // groups, bands), f32),
        in_specs=[
            pl.BlockSpec(memory_space=pltpu.SMEM),
            pl.BlockSpec(memory_space=pltpu.SMEM),
            pl.BlockSpec(memory_space=pltpu.VMEM),
            pl.BlockSpec(memory_space=pl.ANY),
        ],
        out_specs=pl.BlockSpec(memory_space=pltpu.VMEM),
        scratch_shapes=[
            pltpu.VMEM((slots,) + stick, bf16),
            pltpu.VMEM((slots,) + stick, bf16),
            pltpu.VMEM((8, 128), jnp.int32),
            pltpu.VMEM((NX * NZ, 2) + stick, bf16),
            pltpu.VMEM((2, 3, NX, 2) + stick, bf16),
            pltpu.VMEM((2, 3, NX) + stick, bf16),
            pltpu.VMEM((3 * (NZ - 1), 2) + stick, bf16),
            pltpu.VMEM((NX * NZ, 2) + stick, bf16),
            pltpu.VMEM((2, bands, bands), f32),
            pltpu.VMEM((NX - 1, 2, bands // NX, bands), f32),
            pltpu.VMEM((2, bands // NX, bands), f32),
            pltpu.VMEM((NZ, 2, bands // groups, bands), f32),
            dma,
            dma((2,)),
            dma((2,)),
            dma((2, len(HOPS))),
            dma((2, len(HOPS))),
            dma((NX * NZ, 2)),
            dma((NX * NZ, 2)),
            dma((NX - 1,)),
            dma((NX - 1,)),
            dma((NZ,)),
            dma((NZ,)),
        ],
        compiler_params=pltpu.CompilerParams(
            collective_id=0, has_side_effects=True, vmem_limit_bytes=56 * 2**20
        ),
    )(pack, place, count, coefficients.reshape((slots,) + stick))
    return result[None]


def solution(mesh):
    return jax.shard_map(
        local,
        mesh=mesh,
        in_specs=(
            P("pool", "ga", None, None, None),
            P("pool", "ga"),
            P("pool", "ga"),
            P("pool", "ga"),
            P("pool", "ga"),
        ),
        out_specs=P("pool", None, "ga", None),
        check_vma=False,
    )
```

time: 281 us -> 222 us (0.79)
  Pallas kernels: 0 us -> 214 us
  waiting for transfers between devices: 180 us -> 0 us
  local copies, waits for them, and re-layouts: 32.3 us -> 1.92 us
  blocking collectives: 29.2 us -> 0 us
  starting transfers between devices: 19.2 us -> 0 us
  matrix products: 15 us -> 0 us
    pallas_call x0 -> x1, Pallas kernels: none -> 214 us  [local(): pl.pallas_call(functools.partial(kernel, norm_scale), out_shape=jax.Shape...]
    all_to_all x1 -> x0, waiting for transfers between devices: 134 us -> none  [local(): lax.all_to_all(outgoing, 'ga', split_axis=0, concat_axis=0, tiled=True)]
    ppermute x2 -> x0, waiting for transfers between devices: 46.1 us -> none  [passed_along(): return lax.ppermute(value, axis, pairs)]
    all_to_all x1 -> x0, blocking collectives: 29.2 us -> none  [sent_and_summed(): pieces = lax.all_to_all(split_up(x, dim, devices), axis, 0, 0, tiled=True)]
    reshape x3 -> x0, local copies, waits for them, and re-layouts: 26.3 us -> none  [the longest x1 10.6 us: local(): outgoing = outgoing.reshape(groups, pair_cap, -1)]
    dot_general x4 -> x0, matrix products: 15 us -> none  [the longest x1 7.72 us: local(): jnp.dot(packer, coef_rows, preferred_element_type=jnp.float32)]
    all_to_all x1 -> x0, starting transfers between devices: 13.8 us -> none  [local(): lax.all_to_all(outgoing, 'ga', split_axis=0, concat_axis=0, tiled=True)]
    ppermute x2 -> x0, starting transfers between devices: 5.35 us -> none  [passed_along(): return lax.ppermute(value, axis, pairs)]
  transfers between devices with their start and end apart: 3 -> 0, of which waited for: 3 -> 0; matrix products, arithmetic and copies ran while one was open for 2% -> 0% of each run, Pallas kernels for 0% -> 0%
where the time goes in v1:
time: 222 us; the launch traced here: 221 us
  Pallas kernels  214 us (96%)
  other arithmetic  4.39 us (2%)
    pallas_call x1, Pallas kernels, local(): pl.pallas_call(functools.partial(kernel, norm_scale), out_shape=jax.Shape...  214 us

profile of v1, /device:TPU:1, one launch (start us, length us, event | category | flops | bytes accessed | tf_op | source)
XLA Modules:
  0.0 221.2 jit_solution(17777923929944438342)
XLA Ops:
  0.7 0.9 convert_reduce_fusion.1
  1.6 0.7 fusion.1
  2.2 0.7 compare_select_fusion
  2.9 0.7 fusion.3
  3.6 0.2 convert_reduce_fusion
  3.7 0.7 fusion.2
  4.4 0.6 select_reduce_fusion
  5.0 0.6 broadcast_in_dim.52.count_ref
  5.6 214.2 %shard_map.55 = f32[2,8,256]{2,1,0:T(8,128)} custom-call(s32[64]{0:T(128)} %get-tuple-element.6.pack_ref, s32[64]{0:T(128)} %get-tuple-element.5.place_ref, s32[8,128]{1,0:T(8,128)} %broadcast_in_dim.52.count_ref, bf16[32,512,128]{2,1,0:T(8,128)(2,1)} %bitcast.28), custom_call_target="tpu_custom_call" | custom-call | tf_op jit(solution)/shard_map/pallas_call | solution.py:268
  219.9 1.3 copy.8

commit v2 on v1

v2 whole, which is shorter than its diff:
```python
import functools

import jax
import jax.numpy as jnp
from jax import lax
from jax.experimental import pallas as pl
from jax.experimental.pallas import tpu as pltpu
from jax.sharding import PartitionSpec as P

MESH = pl.DeviceIdType.MESH
NX = 4
NZ = 8
WINDOW = 6
GROUP = 64
PARTS = ((0, 192), (192, 64))


def hop_list():
    order = []

    def add(part, dxs, *hops):
        order.extend((part, distance, hop, dx) for distance, hop in hops for dx in dxs)

    far = (2, 1, 3)
    add(0, far, (4, 1), (3, 1), (1, 1), (2, 1), (4, 2), (3, 2), (2, 2), (4, 3), (3, 3), (4, 4))
    add(0, (0,), (4, 1), (3, 1), (2, 1), (4, 2), (3, 2), (2, 2), (4, 3), (3, 3), (4, 4), (1, 1))
    add(1, far, (1, 1), (4, 1), (3, 1), (2, 1), (4, 2), (3, 2), (2, 2))
    add(1, (0,), (4, 1))
    add(1, far, (4, 3))
    add(1, (0,), (3, 1))
    add(1, far, (3, 3))
    add(1, (0,), (4, 2), (3, 2))
    add(1, far, (4, 4))
    add(1, (0,), (2, 1), (4, 3), (3, 3), (1, 1), (2, 2), (4, 4))
    return order


HOPS = hop_list()
RELAY = {(2, 1): 0, (3, 1): 1, (3, 2): 2}


def kernel(
    norm_scale,
    coef_hbm,
    count_hbm,
    device_hbm,
    slot_hbm,
    source_hbm,
    out_ref,
    coef,
    bra,
    maps,
    tables,
    table,
    count_out,
    count_in,
    packed,
    relay,
    relay_half,
    turn,
    final,
    acc,
    x_in,
    rows,
    z_in,
    tail_in,
    load_sem,
    map_sem,
    table_sem,
    bra_sem,
    count_sem,
    hop_send,
    hop_recv,
    x_send,
    x_recv,
    xr_send,
    xr_recv,
    zr_send,
    zr_recv,
    tail_send,
    tail_recv,
):
    pool = lax.axis_index("pool")
    pools = lax.axis_size("pool")
    ga = lax.axis_index("ga")
    x = ga // NZ
    z = lax.rem(ga, NZ)
    after = lax.rem(pool + 1, pools)
    before = lax.rem(pool + pools - 1, pools)

    def at(dx, dz):
        return lax.rem(x + dx, NX) * NZ + lax.rem(z + dz, NZ)

    small = []
    for i, ref in enumerate((device_hbm, slot_hbm, source_hbm, count_hbm)):
        small.append(pltpu.make_async_copy(ref, maps[i], map_sem.at[i]))
        small[-1].start()
    load = pltpu.make_async_copy(coef_hbm, coef, load_sem)
    load.start()
    barrier = pltpu.get_barrier_semaphore()
    greeted = [(pool, at(0, 1)), (pool, at(0, NZ - 1))]
    greeted += [(pool, at(dx, 0)) for dx in range(1, NX)]
    greeted += [(before, ga)] + [(after, at(dx, dz)) for dz in range(NZ) for dx in range(NX)]
    for device in greeted:
        pl.semaphore_signal(barrier, inc=1, device_id=device, device_id_type=MESH)

    for copy in small:
        copy.wait()
    sent = maps[0][...]
    from_stick = maps[2][...]
    slots = sent.shape[1]
    upright = lax.broadcasted_iota(jnp.int32, (slots, slots), 0)
    across = lax.broadcasted_iota(jnp.int32, (slots, slots), 1)

    def standing(row):
        return jnp.sum(jnp.where(upright == across, row, 0), axis=1, keepdims=True)

    def rows_of(devices, order, missing):
        device, key = standing(devices), standing(order)
        earlier = (device == devices) & (order < key)
        rank = jnp.sum(earlier.astype(jnp.int32), axis=1, keepdims=True)
        row = jnp.where(device >= 0, device * 2 + rank, -1)
        lane = lax.broadcasted_iota(jnp.int32, (slots, 128), 1)
        stick = lax.broadcasted_iota(jnp.int32, (slots, 128), 0)
        return jnp.max(jnp.where(row == lane, stick, missing), axis=0, keepdims=True)

    tables[0:1] = rows_of(sent, maps[1][...], 0)
    tables[1:2] = rows_of(
        jnp.where(from_stick >= 0, from_stick // slots, -1), across[:1], -1
    )
    count_out[...] = jnp.broadcast_to(maps[3][...], count_out.shape)
    for total in acc:
        total[...] = jnp.zeros_like(total)
    to_scalars = pltpu.make_async_copy(tables, table, table_sem)
    to_scalars.start()
    load.wait()
    to_scalars.wait()

    def pack_unit(unit, carry):
        target = at(lax.rem(unit, NX), unit // NX)
        for rank in range(2):
            stick = coef[table[0, target * 2 + rank]]
            for part, (first, bands) in enumerate(PARTS):
                packed[part][unit, rank] = stick[:, first : first + bands]
        return carry

    lax.fori_loop(12, 24, pack_unit, 0)
    pl.semaphore_wait(barrier, len(greeted))

    def remote(src, dst, send, recv, device):
        return pltpu.make_async_remote_copy(
            src_ref=src, dst_ref=dst, send_sem=send, recv_sem=recv, device_id=device, device_id_type=MESH
        )

    started = []

    def start(copy):
        copy.start()
        started.append(copy)
        return copy

    def hop_copy(s, n):
        part, distance, hop, dx = HOPS[n]
        dz = distance if s == 0 else NZ - distance
        unit = dz * NX + dx
        half = distance == NZ // 2
        if hop == 1:
            src = packed[part].at[unit, s] if half else packed[part].at[unit]
        elif half:
            src = relay_half[part].at[s, hop - 2, dx]
        else:
            src = relay[part].at[s, RELAY[distance, hop - 1], dx]
        if hop < distance:
            dst = relay_half[part].at[s, hop - 1, dx] if half else relay[part].at[s, RELAY[distance, hop], dx]
        else:
            dst = final[part].at[unit] if dx == 0 else turn[part].at[(dz - 1) * 3 + dx - 1]
            dst = dst.at[s] if half else dst
        return remote(src, dst, hop_send.at[s, n], hop_recv.at[s, n], (pool, at(0, 1 if s == 0 else NZ - 1)))

    hop_copies = [[hop_copy(s, n) for n in range(len(HOPS))] for s in range(2)]
    x_copies = {}

    def x_start(part, dz, dx, s):
        unit = dz * NX + dx
        src = packed[part].at[unit] if dz == 0 else turn[part].at[(dz - 1) * 3 + dx - 1]
        dst = final[part].at[unit]
        if dz == NZ // 2:
            src, dst = src.at[s], dst.at[s]
        sem = (dz * 3 + dx - 1) if s == 0 else 24 + dx - 1
        x_copies[part, dz, dx, s] = start(
            remote(src, dst, x_send.at[part, sem], x_recv.at[part, sem], (pool, at(dx, 0)))
        )

    def multiply(part, first, count, step):
        def one(i, carry):
            unit = first + i * step
            source = lax.rem(x + NX - lax.rem(unit, NX), NX) * NZ + lax.rem(z + NZ - unit // NX, NZ)
            total = None
            for rank in range(2):
                slot = table[1, source * 2 + rank]
                live = (slot >= 0) & (slot < count_in[0, 0])
                mine = bra[jnp.maximum(slot, 0)]
                mine = jnp.where(live, mine, jnp.zeros_like(mine))
                left = jnp.concatenate([mine[0], mine[1]], axis=1)
                ket = final[part][unit, rank]
                plain = jnp.concatenate([ket[0], ket[1]], axis=1)
                swapped = jnp.concatenate([ket[1], -ket[0]], axis=1)
                right = []
                for low in range(0, PARTS[part][1], GROUP):
                    right += [plain[low : low + GROUP], swapped[low : low + GROUP]]
                right = jnp.concatenate(right, axis=0)
                term = lax.dot_general(left, right, (((1,), (1,)), ((), ())), preferred_element_type=jnp.float32)
                total = term if total is None else total + term
            for group in range(PARTS[part][1] // GROUP):
                acc[part][group] += total[:, group * 128 : group * 128 + 128]
            return carry

        lax.fori_loop(0, count, one, 0)

    issued = [0, 0]
    position = {hop: n for n, hop in enumerate(HOPS)}

    def issue(s, arrived):
        while issued[s] < len(HOPS) and issued[s] <= arrived + WINDOW:
            part, distance, hop, dx = HOPS[issued[s]]
            if hop > 1 and position[part, distance, hop - 1, dx] > arrived:
                break
            start(hop_copies[s][issued[s]])
            issued[s] += 1

    for s in range(2):
        issue(s, -1)
    bra_copy = start(remote(coef, bra, bra_sem.at[0], bra_sem.at[1], (after, ga)))
    lax.fori_loop(0, 12, pack_unit, 0)
    lax.fori_loop(24, NX * NZ, pack_unit, 0)
    for part in range(2):
        final[part][0] = packed[part][0]
    count_copy = start(remote(count_out, count_in, count_sem.at[0], count_sem.at[1], (after, ga)))
    three = (2, 1, 3)
    for dx in three:
        x_start(0, 0, dx, 0)

    def wait_x(part, *dzs):
        for dz in dzs:
            for dx in three:
                for s in range(2 if dz == NZ // 2 else 1):
                    x_copies[part, dz, dx, s].wait_recv()

    def to_x():
        copies = []
        for dx in three:
            theirs = pl.ds(pl.multiple_of(lax.rem(x + dx, NX) * 64, 64), 64)
            copies.append(
                start(
                    remote(
                        acc[0].at[:, theirs],
                        x_in.at[dx - 1],
                        xr_send.at[dx - 1],
                        xr_recv.at[dx - 1],
                        (pool, at(dx, 0)),
                    )
                )
            )
        return copies

    def to_z():
        copies = []
        for dz in (4, 3, 5, 2, 6, 1, 7, 0):
            theirs = pl.ds(pl.multiple_of(lax.rem(z + dz, NZ) * 8, 8), 8)
            copies.append(
                start(remote(rows.at[:, theirs], z_in.at[dz], zr_send.at[dz], zr_recv.at[dz], (before, at(0, dz))))
            )
        return copies

    def when(part, distance, hop, dx):
        return position[part, distance, hop, dx]

    for n, (part, distance, hop, dx) in enumerate(HOPS):
        for s in range(2):
            hop_copies[s][n].wait_recv()
            if hop == distance and dx != 0:
                x_start(part, distance if s == 0 else NZ - distance, dx, s if distance == NZ // 2 else 0)
            issue(s, n)
        if n == 11:
            bra_copy.wait_recv()
            count_copy.wait_recv()
            wait_x(0, 0)
            multiply(0, 0, 4, 1)
            multiply(1, 0, 1, 1)
            for d in three:
                x_start(1, 0, d, 0)
        if n == 16:
            wait_x(0, 1, 7)
            multiply(0, 5, 3, 1)
            multiply(0, 29, 3, 1)
        if n == 26:
            wait_x(0, 2, 6)
            multiply(0, 9, 3, 1)
            multiply(0, 25, 3, 1)
            wait_x(1, 0)
            multiply(1, 1, 3, 1)
        if n == 32:
            wait_x(0, 3, 5)
            multiply(0, 13, 3, 1)
            multiply(0, 21, 3, 1)
        if n == 35:
            wait_x(0, 4)
            multiply(0, 17, 3, 1)
        if n == 37:
            multiply(0, 8, 2, 16)
        if n == 38:
            multiply(0, 12, 3, 4)
        if n == 39:
            multiply(0, 4, 2, 24)
            over_x = to_x()
        if n == when(1, 3, 1, 2):
            for copy in over_x:
                copy.wait_recv()
            own = pl.ds(pl.multiple_of(x * 64, 64), 64)
            rows[...] = acc[0][:, own] + x_in[0] + x_in[1] + x_in[2]
        if n == when(1, 3, 1, 1):
            over_z = to_z()
        if n == when(1, 3, 2, 2):
            wait_x(1, 1, 7)
            multiply(1, 5, 3, 1)
            multiply(1, 29, 3, 1)
        if n == when(1, 3, 3, 1):
            wait_x(1, 2, 6)
            multiply(1, 9, 3, 1)
            multiply(1, 25, 3, 1)
        if n == when(1, 3, 3, 0):
            wait_x(1, 3, 5)
            multiply(1, 12, 4, 1)
            multiply(1, 20, 4, 1)
        if n == when(1, 1, 1, 0):
            multiply(1, 4, 2, 24)
            wait_x(1, 4)
            multiply(1, 17, 3, 1)
        if n == when(1, 2, 2, 0):
            multiply(1, 8, 2, 16)
    multiply(1, 16, 1, 1)

    tails = []
    for dz in (4, 3, 5, 2, 6, 1, 7, 0):
        for dx in (2, 1, 3, 0):
            target = at(dx, dz)
            i = dz * NX + dx
            theirs = pl.ds(pl.multiple_of(target * 8, 8), 8)
            tails.append(
                start(
                    remote(acc[1].at[0, theirs], tail_in.at[i], tail_send.at[i], tail_recv.at[i], (before, target))
                )
            )
    for copy in over_z:
        copy.wait_recv()
    result = z_in[0]
    for dz in range(1, NZ):
        result = result + z_in[dz]
    for copy in tails:
        copy.wait_recv()
    last = tail_in[0]
    for i in range(1, NX * NZ):
        last = last + tail_in[i]
    groups = [result[0], result[1], result[2], last]
    for part in range(2):
        lanes = slice(part * GROUP, part * GROUP + GROUP)
        out_ref[part] = jnp.concatenate([group[:, lanes] for group in groups], axis=1) * norm_scale
    for copy in started:
        copy.wait_send()


def local(coefficients, stick_count, dest_device, dest_slot, source_stick):
    groups = lax.axis_size("ga")
    slots = coefficients.shape[1]
    bands = coefficients.shape[3]
    waves = coefficients.shape[4]
    norm_scale = (2 * groups * slots * waves) ** (-0.5)
    stick = (2, bands, waves)
    pieces = [(2, width, waves) for _, width in PARTS]
    bf16, f32 = jnp.bfloat16, jnp.float32
    dma = pltpu.SemaphoreType.DMA
    result = pl.pallas_call(
        functools.partial(kernel, norm_scale),
        out_shape=jax.ShapeDtypeStruct((2, bands // groups, bands), f32),
        in_specs=[
            pl.BlockSpec(memory_space=pl.ANY),
        ] * 5,
        out_specs=pl.BlockSpec(memory_space=pltpu.VMEM),
        scratch_shapes=[
            pltpu.VMEM((slots,) + stick, bf16),
            pltpu.VMEM((slots,) + stick, bf16),
            [pltpu.VMEM((1, width), jnp.int32) for width in (slots, slots, slots, 1)],
            pltpu.VMEM((8, 128), jnp.int32),
            pltpu.SMEM((8, 128), jnp.int32),
            pltpu.VMEM((8, 128), jnp.int32),
            pltpu.VMEM((8, 128), jnp.int32),
            [pltpu.VMEM((NX * NZ, 2) + piece, bf16) for piece in pieces],
            [pltpu.VMEM((2, 3, NX, 2) + piece, bf16) for piece in pieces],
            [pltpu.VMEM((2, 3, NX) + piece, bf16) for piece in pieces],
            [pltpu.VMEM((3 * (NZ - 1), 2) + piece, bf16) for piece in pieces],
            [pltpu.VMEM((NX * NZ, 2) + piece, bf16) for piece in pieces],
            [pltpu.VMEM((width // GROUP, bands, 128), f32) for _, width in PARTS],
            pltpu.VMEM((NX - 1, 3, bands // NX, 128), f32),
            pltpu.VMEM((3, bands // NX, 128), f32),
            pltpu.VMEM((NZ, 3, bands // groups, 128), f32),
            pltpu.VMEM((NX * NZ, bands // groups, 128), f32),
            dma,
            dma((4,)),
            dma,
            dma((2,)),
            dma((2,)),
            dma((2, len(HOPS))),
            dma((2, len(HOPS))),
            dma((2, 27)),
            dma((2, 27)),
            dma((NX - 1,)),
            dma((NX - 1,)),
            dma((NZ,)),
            dma((NZ,)),
            dma((NX * NZ,)),
            dma((NX * NZ,)),
        ],
        compiler_params=pltpu.CompilerParams(
            collective_id=0, has_side_effects=True, vmem_limit_bytes=56 * 2**20
        ),
    )(coefficients.reshape((slots,) + stick), stick_count, dest_device, dest_slot, source_stick)
    return result[None]


def solution(mesh):
    return jax.shard_map(
        local,
        mesh=mesh,
        in_specs=(
            P("pool", "ga", None, None, None),
            P("pool", "ga"),
            P("pool", "ga"),
            P("pool", "ga"),
            P("pool", "ga"),
        ),
        out_specs=P("pool", None, "ga", None),
        check_vma=False,
    )
```

time: 222 us -> 214 us (0.964)
  other arithmetic: 4.39 us -> 0 us
  Pallas kernels: 214 us -> 211 us
    pallas_call x1, Pallas kernels: 214 us -> 211 us  [local(): pl.pallas_call(functools.partial(kernel, norm_scale), out_shape=jax.Shape...]
where the time goes in v2:
time: 214 us; the launch traced here: 213 us
  Pallas kernels  211 us (99%)
    pallas_call x1, Pallas kernels, local(): pl.pallas_call(functools.partial(kernel, norm_scale), out_shape=jax.Shape...  211 us

profile of v2, /device:TPU:1, one launch (start us, length us, event | category | flops | bytes accessed | tf_op | source)
XLA Modules:
  0.0 212.9 jit_solution(4561030947149105754)
XLA Ops:
  0.7 211.0 %shard_map.55 = f32[2,8,256]{2,1,0:T(8,128)} custom-call(bf16[32,2,256,128]{3,2,1,0:T(8,128)(2,1)} %bitcast.2, s32[1,1]{1,0:T(1,128)S(6)} %copy.7.count_hbm, s32[1,32]{1,0:T(1,128)} %device_hbm.1, s32[1,32]{1,0:T(1,128)} %slot_hbm.1, s32[1,32]{1,0:T(1,128)} %source_hbm.1), custom_call_target="tpu_custom_call" | custom-call | tf_op jit(solution)/shard_map/pallas_call | solution.py:382
  211.6 1.3 copy.8

commit v3 on v2

--- a/solution.py
+++ b/solution.py
@@ -12,6 +12,7 @@
 NZ = 8
 WINDOW = 6
 GROUP = 64
+ALL = -1
 PARTS = ((0, 192), (192, 64))
 
 
@@ -24,13 +25,13 @@
     far = (2, 1, 3)
     add(0, far, (4, 1), (3, 1), (1, 1), (2, 1), (4, 2), (3, 2), (2, 2), (4, 3), (3, 3), (4, 4))
     add(0, (0,), (4, 1), (3, 1), (2, 1), (4, 2), (3, 2), (2, 2), (4, 3), (3, 3), (4, 4), (1, 1))
-    add(1, far, (1, 1), (4, 1), (3, 1), (2, 1), (4, 2), (3, 2), (2, 2))
+    add(1, (ALL,), (1, 1), (4, 1), (3, 1), (2, 1), (4, 2), (3, 2), (2, 2))
     add(1, (0,), (4, 1))
-    add(1, far, (4, 3))
+    add(1, (ALL,), (4, 3))
     add(1, (0,), (3, 1))
-    add(1, far, (3, 3))
+    add(1, (ALL,), (3, 3))
     add(1, (0,), (4, 2), (3, 2))
-    add(1, far, (4, 4))
+    add(1, (ALL,), (4, 4))
     add(1, (0,), (2, 1), (4, 3), (3, 3), (1, 1), (2, 2), (4, 4))
     return order
 
@@ -144,7 +145,7 @@
                 packed[part][unit, rank] = stick[:, first : first + bands]
         return carry
 
-    lax.fori_loop(12, 24, pack_unit, 0)
+    lax.fori_loop(16, 20, pack_unit, 0)
     pl.semaphore_wait(barrier, len(greeted))
 
     def remote(src, dst, send, recv, device):
@@ -163,18 +164,21 @@
         part, distance, hop, dx = HOPS[n]
         dz = distance if s == 0 else NZ - distance
         unit = dz * NX + dx
+        lane, corner = dx, (dz - 1) * 3 + dx - 1
+        if dx == ALL:
+            unit, lane, corner = pl.ds(dz * NX + 1, 3), pl.ds(1, 3), pl.ds((dz - 1) * 3, 3)
         half = distance == NZ // 2
         if hop == 1:
             src = packed[part].at[unit, s] if half else packed[part].at[unit]
         elif half:
-            src = relay_half[part].at[s, hop - 2, dx]
+            src = relay_half[part].at[s, hop - 2, lane]
         else:
-            src = relay[part].at[s, RELAY[distance, hop - 1], dx]
+            src = relay[part].at[s, RELAY[distance, hop - 1], lane]
         if hop < distance:
-            dst = relay_half[part].at[s, hop - 1, dx] if half else relay[part].at[s, RELAY[distance, hop], dx]
+            dst = relay_half[part].at[s, hop - 1, lane] if half else relay[part].at[s, RELAY[distance, hop], lane]
         else:
-            dst = final[part].at[unit] if dx == 0 else turn[part].at[(dz - 1) * 3 + dx - 1]
-            dst = dst.at[s] if half else dst
+            over, place = (final, unit) if dx == 0 else (turn, corner)
+            dst = over[part].at[place, s] if half else over[part].at[place]
         return remote(src, dst, hop_send.at[s, n], hop_recv.at[s, n], (pool, at(0, 1 if s == 0 else NZ - 1)))
 
     hop_copies = [[hop_copy(s, n) for n in range(len(HOPS))] for s in range(2)]
@@ -229,10 +233,19 @@
             issued[s] += 1
 
     for s in range(2):
+        for _ in range(3):
+            start(hop_copies[s][issued[s]])
+            issued[s] += 1
+    lax.fori_loop(12, 16, pack_unit, 0)
+    lax.fori_loop(20, 24, pack_unit, 0)
+    lax.fori_loop(4, 8, pack_unit, 0)
+    lax.fori_loop(28, 32, pack_unit, 0)
+    for s in range(2):
         issue(s, -1)
     bra_copy = start(remote(coef, bra, bra_sem.at[0], bra_sem.at[1], (after, ga)))
-    lax.fori_loop(0, 12, pack_unit, 0)
-    lax.fori_loop(24, NX * NZ, pack_unit, 0)
+    lax.fori_loop(0, 4, pack_unit, 0)
+    lax.fori_loop(8, 12, pack_unit, 0)
+    lax.fori_loop(24, 28, pack_unit, 0)
     for part in range(2):
         final[part][0] = packed[part][0]
     count_copy = start(remote(count_out, count_in, count_sem.at[0], count_sem.at[1], (after, ga)))
@@ -279,7 +292,8 @@
         for s in range(2):
             hop_copies[s][n].wait_recv()
             if hop == distance and dx != 0:
-                x_start(part, distance if s == 0 else NZ - distance, dx, s if distance == NZ // 2 else 0)
+                for d in three if dx == ALL else (dx,):
+                    x_start(part, distance if s == 0 else NZ - distance, d, s if distance == NZ // 2 else 0)
             issue(s, n)
         if n == 11:
             bra_copy.wait_recv()
@@ -313,18 +327,18 @@
         if n == 39:
             multiply(0, 4, 2, 24)
             over_x = to_x()
-        if n == when(1, 3, 1, 2):
+        if n == when(1, 3, 1, ALL):
             for copy in over_x:
                 copy.wait_recv()
             own = pl.ds(pl.multiple_of(x * 64, 64), 64)
             rows[...] = acc[0][:, own] + x_in[0] + x_in[1] + x_in[2]
-        if n == when(1, 3, 1, 1):
+        if n == when(1, 4, 4, ALL):
             over_z = to_z()
-        if n == when(1, 3, 2, 2):
+        if n == when(1, 3, 2, ALL):
             wait_x(1, 1, 7)
             multiply(1, 5, 3, 1)
             multiply(1, 29, 3, 1)
-        if n == when(1, 3, 3, 1):
+        if n == when(1, 3, 3, ALL):
             wait_x(1, 2, 6)
             multiply(1, 9, 3, 1)
             multiply(1, 25, 3, 1)
@@ -340,6 +354,7 @@
             multiply(1, 8, 2, 16)
     multiply(1, 16, 1, 1)
 
+    earlier = len(started)
     tails = []
     for dz in (4, 3, 5, 2, 6, 1, 7, 0):
         for dx in (2, 1, 3, 0):
@@ -351,6 +366,8 @@
                     remote(acc[1].at[0, theirs], tail_in.at[i], tail_send.at[i], tail_recv.at[i], (before, target))
                 )
             )
+    for copy in started[:earlier]:
+        copy.wait_send()
     for copy in over_z:
         copy.wait_recv()
     result = z_in[0]
@@ -364,8 +381,8 @@
     groups = [result[0], result[1], result[2], last]
     for part in range(2):
         lanes = slice(part * GROUP, part * GROUP + GROUP)
-        out_ref[part] = jnp.concatenate([group[:, lanes] for group in groups], axis=1) * norm_scale
-    for copy in started:
+        out_ref[part] = jnp.concatenate([group[:, lanes] for group in groups], axis=1)
+    for copy in tails:
         copy.wait_send()
 
 
@@ -424,7 +441,7 @@
             collective_id=0, has_side_effects=True, vmem_limit_bytes=56 * 2**20
         ),
     )(coefficients.reshape((slots,) + stick), stick_count, dest_device, dest_slot, source_stick)
-    return result[None]
+    return result[None] * norm_scale
 
 
 def solution(mesh):

time: 214 us -> 212 us (level)
  no operation moved by 1% of the time
where the time goes in v3:
time: 212 us
  Pallas kernels  210 us (99%)
    pallas_call x1, Pallas kernels, local(): pl.pallas_call(functools.partial(kernel, norm_scale), out_shape=jax.Shape...  210 us

profile of v3, /device:TPU:1, one launch (start us, length us, event | category | flops | bytes accessed | tf_op | source)
XLA Modules:
  0.0 211.7 jit_solution(11835847496105734505)
XLA Ops:
  0.7 209.8 %shard_map.55 = f32[2,8,256]{2,1,0:T(8,128)} custom-call(bf16[32,2,256,128]{3,2,1,0:T(8,128)(2,1)} %bitcast.3, s32[1,1]{1,0:T(1,128)S(6)} %copy.6.count_hbm, s32[1,32]{1,0:T(1,128)} %device_hbm.1, s32[1,32]{1,0:T(1,128)} %slot_hbm.1, s32[1,32]{1,0:T(1,128)} %source_hbm.1), custom_call_target="tpu_custom_call" | custom-call | tf_op jit(solution)/shard_map/pallas_call | solution.py:399
  210.4 1.3 multiply_bitcast_fusion

commit v4 on v3

--- a/solution.py
+++ b/solution.py
@@ -22,8 +22,7 @@
     def add(part, dxs, *hops):
         order.extend((part, distance, hop, dx) for distance, hop in hops for dx in dxs)
 
-    far = (2, 1, 3)
-    add(0, far, (4, 1), (3, 1), (1, 1), (2, 1), (4, 2), (3, 2), (2, 2), (4, 3), (3, 3), (4, 4))
+    add(0, (ALL,), (4, 1), (3, 1), (1, 1), (2, 1), (4, 2), (3, 2), (2, 2), (4, 3), (3, 3), (4, 4))
     add(0, (0,), (4, 1), (3, 1), (2, 1), (4, 2), (3, 2), (2, 2), (4, 3), (3, 3), (4, 4), (1, 1))
     add(1, (ALL,), (1, 1), (4, 1), (3, 1), (2, 1), (4, 2), (3, 2), (2, 2))
     add(1, (0,), (4, 1))
@@ -233,19 +232,19 @@
             issued[s] += 1
 
     for s in range(2):
-        for _ in range(3):
+        for _ in range(1):
             start(hop_copies[s][issued[s]])
             issued[s] += 1
     lax.fori_loop(12, 16, pack_unit, 0)
     lax.fori_loop(20, 24, pack_unit, 0)
     lax.fori_loop(4, 8, pack_unit, 0)
     lax.fori_loop(28, 32, pack_unit, 0)
+    lax.fori_loop(8, 12, pack_unit, 0)
+    lax.fori_loop(24, 28, pack_unit, 0)
     for s in range(2):
         issue(s, -1)
     bra_copy = start(remote(coef, bra, bra_sem.at[0], bra_sem.at[1], (after, ga)))
     lax.fori_loop(0, 4, pack_unit, 0)
-    lax.fori_loop(8, 12, pack_unit, 0)
-    lax.fori_loop(24, 28, pack_unit, 0)
     for part in range(2):
         final[part][0] = packed[part][0]
     count_copy = start(remote(count_out, count_in, count_sem.at[0], count_sem.at[1], (after, ga)))
@@ -295,7 +294,7 @@
                 for d in three if dx == ALL else (dx,):
                     x_start(part, distance if s == 0 else NZ - distance, d, s if distance == NZ // 2 else 0)
             issue(s, n)
-        if n == 11:
+        if n == 3:
             bra_copy.wait_recv()
             count_copy.wait_recv()
             wait_x(0, 0)
@@ -303,28 +302,28 @@
             multiply(1, 0, 1, 1)
             for d in three:
                 x_start(1, 0, d, 0)
-        if n == 16:
+        if n == 5:
             wait_x(0, 1, 7)
             multiply(0, 5, 3, 1)
             multiply(0, 29, 3, 1)
-        if n == 26:
+        if n == 8:
             wait_x(0, 2, 6)
             multiply(0, 9, 3, 1)
             multiply(0, 25, 3, 1)
             wait_x(1, 0)
             multiply(1, 1, 3, 1)
-        if n == 32:
+        if n == 12:
             wait_x(0, 3, 5)
             multiply(0, 13, 3, 1)
             multiply(0, 21, 3, 1)
-        if n == 35:
+        if n == 15:
             wait_x(0, 4)
             multiply(0, 17, 3, 1)
-        if n == 37:
+        if n == 17:
             multiply(0, 8, 2, 16)
-        if n == 38:
+        if n == 18:
             multiply(0, 12, 3, 4)
-        if n == 39:
+        if n == 19:
             multiply(0, 4, 2, 24)
             over_x = to_x()
         if n == when(1, 3, 1, ALL):

time: 212 us -> 212 us (level)
  no operation moved by 1% of the time
where the time goes in v4:
time: 212 us; the launch traced here: 211 us
  Pallas kernels  209 us (99%)
    pallas_call x1, Pallas kernels, local(): pl.pallas_call(functools.partial(kernel, norm_scale), out_shape=jax.Shape...  209 us

profile of v4, /device:TPU:1, one launch (start us, length us, event | category | flops | bytes accessed | tf_op | source)
XLA Modules:
  0.0 211.0 jit_solution(1808249875318971196)
XLA Ops:
  0.7 209.0 %shard_map.55 = f32[2,8,256]{2,1,0:T(8,128)} custom-call(bf16[32,2,256,128]{3,2,1,0:T(8,128)(2,1)} %bitcast.3, s32[1,1]{1,0:T(1,128)S(6)} %copy.6.count_hbm, s32[1,32]{1,0:T(1,128)} %device_hbm.1, s32[1,32]{1,0:T(1,128)} %slot_hbm.1, s32[1,32]{1,0:T(1,128)} %source_hbm.1), custom_call_target="tpu_custom_call" | custom-call | tf_op jit(solution)/shard_map/pallas_call | solution.py:398
  209.7 1.3 multiply_bitcast_fusion
